TPU v7x, 8 devices: a whole 2x2x1 slice. The times are simulated.
8 devices in a mesh: mp: 1 (over z), dpa: 2 (over y), dpb: 2 (over x), dpc: 2 (over core).
Axes of the slice: x: 2, y: 2, z: 1, core: 2. Of those that a mesh axis runs over, the one named last changes fastest.
Arguments:
- x: bfloat16 [8192, 2048], P(('mp', 'dpa', 'dpb', 'dpc'))
- g: bfloat16 [8192, 2048], P(('mp', 'dpa', 'dpb', 'dpc'))
- w1: bfloat16 [2048, 8192], P('mp')
- w2: bfloat16 [8192, 2048], P('mp')
- w3: bfloat16 [2048, 8192], P('mp')
- w4: bfloat16 [8192, 2048], P('mp')
Outputs:
- output 1: float32 [2048, 8192], P('mp')
- output 2: float32 [8192, 2048], P('mp')
- output 3: float32 [2048, 8192], P('mp')
- output 4: float32 [8192, 2048], P('mp')
- output 5: bfloat16 [8192, 2048], P(('mp', 'dpa', 'dpb', 'dpc'))
All inputs are finite; a program needn't handle non-finite values.
Results may differ from a plain program's by a relative error of at most 0.0114265.
Values are sent between devices in bfloat16 or wider.
A program may use at most 1.75 GiB of HBM per device.

v0:
```python
import jax
import jax.numpy as jnp
from jax import lax
from jax.sharding import PartitionSpec as P


def gelu_grad(a, d):
    return jax.vjp(lambda t: jax.nn.gelu(t, approximate=True), a)[1](d)[0]


def solution(mesh):
    ndev = mesh.shape["dpa"] * mesh.shape["dpb"] * mesh.shape["dpc"]
    f32 = jnp.float32
    bf = jnp.bfloat16
    rows = P(("mp", "dpa", "dpb", "dpc"), None)
    wspec = P("mp", None)

    def reduce_grad(dw):
        s = lax.psum_scatter(dw, "dpc", scatter_dimension=0, tiled=True)
        s = lax.psum(s, ("dpa", "dpb"))
        return lax.all_gather(s, "dpc", axis=0, tiled=True) / ndev

    def local(x, g, w1, w2, w3, w4):
        a1 = jnp.dot(x, w1, preferred_element_type=f32).astype(bf)
        h1 = jax.nn.gelu(a1.astype(f32), approximate=True).astype(bf)
        h2 = (jnp.dot(h1, w2, preferred_element_type=f32) + x.astype(f32)).astype(bf)
        a3 = jnp.dot(h2, w3, preferred_element_type=f32).astype(bf)
        h3 = jax.nn.gelu(a3.astype(f32), approximate=True).astype(bf)
        dw4 = reduce_grad(jnp.dot(h3.T, g, preferred_element_type=f32))
        dh3 = jnp.dot(g, w4.T, preferred_element_type=f32).astype(bf)
        da3 = gelu_grad(a3.astype(f32), dh3.astype(f32)).astype(bf)
        dw3 = reduce_grad(jnp.dot(h2.T, da3, preferred_element_type=f32))
        dh2 = (jnp.dot(da3, w3.T, preferred_element_type=f32) + g.astype(f32)).astype(bf)
        dw2 = reduce_grad(jnp.dot(h1.T, dh2, preferred_element_type=f32))
        dh1 = jnp.dot(dh2, w2.T, preferred_element_type=f32).astype(bf)
        da1 = gelu_grad(a1.astype(f32), dh1.astype(f32)).astype(bf)
        dw1 = reduce_grad(jnp.dot(x.T, da1, preferred_element_type=f32))
        dx = (jnp.dot(da1, w1.T, preferred_element_type=f32) + dh2.astype(f32)).astype(bf)
        return dw1, dw2, dw3, dw4, dx

    return jax.shard_map(local, mesh=mesh, in_specs=(rows, rows, wspec, wspec, wspec, wspec), out_specs=(wspec, wspec, wspec, wspec, rows), check_vma=False)
```

profile of v0, /device:TPU:0, one launch (start us, length us, event | category | flops | bytes accessed | tf_op | source)
XLA Modules:
  0.0 3323.0 jit_solution(3555132125398940529)
XLA Ops:
  7.2 0.0 reduce-scatter.11.cloned.1.call-start
  7.2 41.9 %convolution_convert_fusion.1 = bf16[1024,8192]{1,0:T(8,128)(2,1)} fusion(bf16[1024,2048]{1,0:T(8,128)(2,1)} %param.6, bf16[2048,8192]{1,0:T(8,128)(2,1)} %param.8), kind=kOutput, calls=%fused_computation.45 | convolution fusion | flops 34368126976 | bytes 54525952 | tf_op jit(solution)/shard_map/dot_general | solution.py:24
  49.1 52.5 %add_convert_fusion.2 = bf16[1024,2048]{1,0:T(8,128)(2,1)} fusion(bf16[1024,2048]{1,0:T(8,128)(2,1)} %param.6, bf16[8192,2048]{1,0:T(8,128)(2,1)} %param.9, bf16[1024,8192]{1,0:T(8,128)(2,1)} %convolution_convert_fusion.1), kind=kOutput, calls=%fused_computation.48 | convolution fusion | flops 34449915904 | bytes 58720256 | tf_op jit(solution)/shard_map/dot_general | solution.py:26
  101.6 42.3 %convolution_convert_fusion = bf16[1024,8192]{1,0:T(8,128)(2,1)} fusion(bf16[1024,2048]{1,0:T(8,128)(2,1)} %add_convert_fusion.2, bf16[2048,8192]{1,0:T(8,128)(2,1)} %param.10), kind=kOutput, calls=%fused_computation.44 | convolution fusion | flops 34368126976 | bytes 54525952 | tf_op jit(solution)/shard_map/dot_general | solution.py:27
  143.9 51.7 %fusion.22 = f32[8192,2048]{1,0:T(8,128)} fusion(bf16[1024,2048]{1,0:T(8,128)(2,1)S(1)} %copy-done, bf16[1024,8192]{1,0:T(8,128)(2,1)} %convolution_convert_fusion), kind=kOutput, calls=%fused_computation.39 | convolution fusion | flops 34443624448 | bytes 88080384 | tf_op jit(solution)/shard_map/dot_general | solution.py:29
  195.6 0.0 reduce-scatter.7.cloned.1.call-start
  195.6 63.0 %fusion.4 = bf16[1024,8192]{1,0:T(8,128)(2,1)} fusion(bf16[1024,8192]{1,0:T(8,128)(2,1)} %convolution_convert_fusion, bf16[1024,2048]{1,0:T(8,128)(2,1)} %param.7, bf16[8192,2048]{1,0:T(8,128)(2,1)} %param.11), kind=kOutput, calls=%fused_computation.17 | convolution fusion | flops 34552676352 | bytes 71303168 | tf_op jit(solution)/shard_map/dot_general | solution.py:30
  258.6 51.1 %add_convert_fusion.1 = bf16[1024,2048]{1,0:T(8,128)(2,1)} fusion(bf16[1024,2048]{1,0:T(8,128)(2,1)} %param.7, bf16[1024,8192]{1,0:T(8,128)(2,1)} %fusion.4, bf16[2048,8192]{1,0:T(8,128)(2,1)} %param.10), kind=kOutput, calls=%fused_computation.47 | convolution fusion | flops 34366029824 | bytes 58720256 | tf_op jit(solution)/shard_map/dot_general | solution.py:33
  309.7 52.7 %fusion.32 = f32[8192,2048]{1,0:T(8,128)} fusion(bf16[1024,2048]{1,0:T(8,128)(2,1)} %add_convert_fusion.1, bf16[1024,8192]{1,0:T(8,128)(2,1)} %convolution_convert_fusion.1), kind=kOutput, calls=%fused_computation.53 | convolution fusion | flops 34443624448 | bytes 88080384 | tf_op jit(solution)/shard_map/dot_general | solution.py:34
  362.4 0.0 reduce-scatter.9.cloned.1.call-start
  362.5 54.4 %fusion.35 = f32[2048,8192]{0,1:T(8,128)} fusion(bf16[1024,2048]{1,0:T(8,128)(2,1)} %add_convert_fusion.2, bf16[1024,8192]{1,0:T(8,128)(2,1)} %fusion.4), kind=kOutput, calls=%fused_computation.54 | convolution fusion | flops 34359738368 | bytes 88080384 | tf_op jit(solution)/shard_map/dot_general | solution.py:32
  416.8 0.0 reduce-scatter.5.cloned.1.call-start
  416.9 66.7 %fusion.7 = bf16[1024,8192]{1,0:T(8,128)(2,1)} fusion(bf16[1024,8192]{1,0:T(8,128)(2,1)} %convolution_convert_fusion.1, bf16[1024,2048]{1,0:T(8,128)(2,1)} %add_convert_fusion.1, bf16[8192,2048]{1,0:T(8,128)(2,1)} %param.9), kind=kOutput, calls=%fused_computation.20 | convolution fusion | flops 34552676352 | bytes 71303168 | tf_op jit(solution)/shard_map/dot_general | solution.py:35
  483.6 49.1 %convolution_bitcast_fusion = f32[2048,8192]{0,1:T(8,128)} fusion(bf16[1024,8192]{1,0:T(8,128)(2,1)} %fusion.7, bf16[1024,2048]{1,0:T(8,128)(2,1)} %param.6), kind=kOutput, calls=%fused_computation.14 | convolution fusion | flops 34359738368 | bytes 88080384 | tf_op jit(solution)/shard_map/dot_general | solution.py:37
  532.7 0.0 all-reduce.4.cloned.1.call-start
  532.8 0.5 all-reduce.4.cloned.1.call-update
  533.3 0.0 all-reduce.6.cloned.1.call-start
  533.4 76.4 %reduce-scatter.5.cloned.1.call-done = f32[1024,8192]{0,1:T(8,128)} async-done(((f32[2048,8192]{0,1:T(8,128)}), f32[1024,8192]{0,1:T(8,128)}) %reduce-scatter.5.cloned.1.call-update) | async-done | bytes 33554448 | tf_op jit(solution)/shard_map/reduce_scatter | solution.py:19
  609.9 571.2 %all-reduce.4.cloned.1.call-done = f32[4096,2048]{1,0:T(8,128)} async-done(((f32[4096,2048]{1,0:T(8,128)}), f32[4096,2048]{1,0:T(8,128)}) %all-reduce.4.cloned.1.call-update) | async-done | bytes 33554448 | tf_op jit(solution)/shard_map/psum | solution.py:20
  1181.2 1658.2 %all-reduce.6.cloned.1.call-done = (f32[1024,8192]{0,1:T(8,128)}, f32[4096,2048]{1,0:T(8,128)}, f32[1024,8192]{0,1:T(8,128)}) async-done(((f32[1024,8192]{0,1:T(8,128)}, f32[4096,2048]{1,0:T(8,128)}, f32[1024,8192]{0,1:T(8,128)}), (f32[1024,8192]{0,1:T(8,128)}, f32[4096,2048]{1,0:T(8,128)}, f32[1024,8192]{0,1:T(8,128)})) %all-reduce.6.cloned.1.call-update) | async-done | bytes 100663312 | tf_op jit(solution)/shard_map/psum | solution.py:20
  2839.5 0.7 all-gather.9.cloned.1.call-update
  2840.2 0.0 all-gather.7.cloned.1.call-start
  2840.2 0.5 all-gather.7.cloned.1.call-update
  2840.8 48.4 %add_convert_fusion = bf16[1024,2048]{1,0:T(8,128)(2,1)} fusion(bf16[1024,2048]{1,0:T(8,128)(2,1)} %add_convert_fusion.1, bf16[1024,8192]{1,0:T(8,128)(2,1)} %fusion.7, bf16[2048,8192]{1,0:T(8,128)(2,1)} %param.8), kind=kOutput, calls=%fused_computation.46 | convolution fusion | flops 34366029824 | bytes 58720256 | tf_op jit(solution)/shard_map/dot_general | solution.py:38
  2889.2 46.2 %all-gather.11.cloned.1.call-done = f32[8192,2048]{1,0:T(8,128)} async-done(((f32[4096,2048]{1,0:T(8,128)}), f32[8192,2048]{1,0:T(8,128)}) %all-gather.11.cloned.1.call-update) | async-done | bytes 67108880 | tf_op jit(solution)/shard_map/all_gather | solution.py:21
  2935.3 60.3 %broadcast_multiply_fusion = f32[8192,2048]{1,0:T(8,128)} fusion(f32[8192,2048]{1,0:T(8,128)} %all-gather.11.cloned.1.call-done), kind=kLoop, calls=%fused_computation.35 | loop fusion | flops 16777216 | bytes 134217728 | tf_op jit(solution)/shard_map/div | solution.py:21
  2995.7 34.5 %all-gather.5.cloned.1.call-done = f32[2048,8192]{0,1:T(8,128)} async-done(((f32[1024,8192]{0,1:T(8,128)}), f32[2048,8192]{0,1:T(8,128)}) %all-gather.5.cloned.1.call-update) | async-done | bytes 67108880 | tf_op jit(solution)/shard_map/all_gather | solution.py:21
  3030.2 60.4 %broadcast_multiply_fusion.3 = f32[2048,8192]{0,1:T(8,128)} fusion(f32[2048,8192]{0,1:T(8,128)} %all-gather.5.cloned.1.call-done), kind=kLoop, calls=%fused_computation.38 | loop fusion | flops 16777216 | bytes 134217728 | tf_op jit(solution)/shard_map/div | solution.py:21
  3090.5 67.3 %copy.12 = f32[2048,8192]{1,0:T(8,128)} copy(f32[2048,8192]{0,1:T(8,128)} %broadcast_multiply_fusion.3) | data formatting | bytes 134217728
  3157.9 53.3 %broadcast_multiply_fusion.2 = f32[2048,8192]{0,1:T(8,128)} fusion(f32[2048,8192]{0,1:T(8,128)} %all-gather.9.cloned.1.call-done), kind=kLoop, calls=%fused_computation.37 | loop fusion | flops 16777216 | bytes 134217728 | tf_op jit(solution)/shard_map/div | solution.py:21
  3211.2 61.2 %copy.13 = f32[2048,8192]{1,0:T(8,128)} copy(f32[2048,8192]{0,1:T(8,128)} %broadcast_multiply_fusion.2) | data formatting | bytes 134217728
  3272.4 43.6 %broadcast_multiply_fusion.1 = f32[8192,2048]{1,0:T(8,128)} fusion(f32[8192,2048]{1,0:T(8,128)} %all-gather.7.cloned.1.call-done), kind=kLoop, calls=%fused_computation.36 | loop fusion | flops 16777216 | bytes 134217728 | tf_op jit(solution)/shard_map/div | solution.py:21
  (17 shorter events, 0.3 us)
Async XLA Ops:
  7.2 525.6 %reduce-scatter.11.cloned.1.call-start = ((), (), s32[]{:S(2)}) async-start(), calls=%async_computation.10 | async-start | bytes 100663296 | tf_op jit(solution)/shard_map/reduce_scatter | solution.py:19
  101.6 42.3 %copy-start = (bf16[1024,2048]{1,0:T(8,128)(2,1)S(1)}, bf16[1024,2048]{1,0:T(8,128)(2,1)}, u32[]{:S(2)}) copy-start(bf16[1024,2048]{1,0:T(8,128)(2,1)} %param.7) | copy-start | bytes 12582916
  195.6 337.8 %reduce-scatter.7.cloned.1.call-start = ((), (), s32[]{:S(2)}) async-start(), calls=%async_computation.6 | async-start | bytes 100663296 | tf_op jit(solution)/shard_map/reduce_scatter | solution.py:19
  362.4 171.0 %reduce-scatter.9.cloned.1.call-start = ((), (), s32[]{:S(2)}) async-start(), calls=%async_computation.8 | async-start | bytes 100663296 | tf_op jit(solution)/shard_map/reduce_scatter | solution.py:19
  416.8 193.0 %reduce-scatter.5.cloned.1.call-start = ((), (), s32[]{:S(2)}) async-start(), calls=%async_computation.4 | async-start | bytes 100663296 | tf_op jit(solution)/shard_map/reduce_scatter | solution.py:19
  532.7 648.4 %all-reduce.4.cloned.1.call-start = ((), (), s32[]{:S(2)}) async-start(), calls=%async_computation.11 | async-start | bytes 67108864 | tf_op jit(solution)/shard_map/psum | solution.py:20
  533.3 2306.1 %all-reduce.6.cloned.1.call-start = ((), (), s32[]{:S(2)}) async-start(), calls=%async_computation.13 | async-start | bytes 201326592 | tf_op jit(solution)/shard_map/psum | solution.py:20
  609.8 2325.5 %all-gather.11.cloned.1.call-start = ((), (), s32[]{:S(2)}) async-start(), calls=%async_computation.12 | async-start | bytes 100663296 | tf_op jit(solution)/shard_map/all_gather | solution.py:21
  1181.2 1849.0 %all-gather.5.cloned.1.call-start = ((), (), s32[]{:S(2)}) async-start(), calls=%async_computation.5 | async-start | bytes 100663296 | tf_op jit(solution)/shard_map/all_gather | solution.py:21
  2839.4 318.4 %all-gather.9.cloned.1.call-start = ((), (), s32[]{:S(2)}) async-start(), calls=%async_computation.9 | async-start | bytes 100663296 | tf_op jit(solution)/shard_map/all_gather | solution.py:21
  2840.2 432.2 %all-gather.7.cloned.1.call-start = ((), (), s32[]{:S(2)}) async-start(), calls=%async_computation.7 | async-start | bytes 100663296 | tf_op jit(solution)/shard_map/all_gather | solution.py:21
Sparse Core Ops, SparseCore 0:
  195.7 77.1 reduce-scatter.10
  362.5 76.9 reduce-scatter.6
  442.4 75.6 reduce-scatter.8
  532.9 76.9 reduce-scatter.4
  613.2 567.8 all-reduce.3
  1185.0 1654.4 all-reduce.5
  2840.9 94.3 all-gather.10
  2936.9 93.2 all-gather.4
  3031.7 93.2 all-gather.8
  3126.4 93.2 all-gather.6
where the time goes:
time: 3330 us; the launch traced here: 3320 us
  waiting for transfers between devices  2390 us (72%)
  matrix products  574 us (17%)
  other arithmetic  218 us (7%)
  local copies, waits for them, and re-layouts  129 us (4%)
    psum x2, waiting for transfers between devices, reduce_grad(): s = lax.psum(s, ('dpa', 'dpb'))  2230 us
    div x4, other arithmetic, reduce_grad(): return lax.all_gather(s, 'dpc', axis=0, tiled=True) / ndev  218 us
    unnamed x4, local copies, waits for them, and re-layouts  129 us
    all_gather x4, waiting for transfers between devices, reduce_grad(): return lax.all_gather(s, 'dpc', axis=0, tiled=True) / ndev  80.7 us
    reduce_scatter x4, waiting for transfers between devices, reduce_grad(): s = lax.psum_scatter(dw, 'dpc', scatter_dimension=0, tiled=True)  76.4 us
    dot_general x1, matrix products, local(): dh1 = jnp.dot(dh2, w2.T, preferred_element_type=f32).astype(bf)  66.7 us
  transfers between devices with their start and end apart: 10, of which 5 were waited for; matrix products, arithmetic and copies ran while one was open for 21% of the time, Pallas kernels for 0%

commit v1 on v0

v1 whole, which is shorter than its diff:
```python
import jax
import jax.numpy as jnp
from jax import lax
from jax.sharding import PartitionSpec as P


GROUP = ("dpa", "dpb", "dpc")
f32 = jnp.float32
bf = jnp.bfloat16


def gelu(a):
    return jax.nn.gelu(a.astype(f32), approximate=True).astype(bf)


def gelu_grad(a, d):
    return jax.vjp(lambda t: jax.nn.gelu(t, approximate=True), a.astype(f32))[1](d.astype(f32))[0].astype(bf)


def nn(a, b):
    return jnp.dot(a, b, preferred_element_type=f32)


def nt(a, b):
    return lax.dot_general(a, b, (((1,), (1,)), ((), ())), preferred_element_type=f32)


def tn(a, b):
    return lax.dot_general(a, b, (((0,), (0,)), ((), ())), preferred_element_type=f32)


def solution(mesh):
    ndev = mesh.shape["dpa"] * mesh.shape["dpb"] * mesh.shape["dpc"]
    ncore = mesh.shape["dpc"]
    rows = P(("mp",) + GROUP, None)
    wspec = P("mp", None)

    def swap(v):
        return lax.ppermute(v, "dpc", [(i, ncore - 1 - i) for i in range(ncore)])

    def join(mine, theirs, axis):
        core = lax.axis_index("dpc")
        n = mine.shape[axis]
        shape = list(mine.shape)
        shape[axis] = 2 * n
        out = jnp.zeros(shape, mine.dtype)
        out = lax.dynamic_update_slice_in_dim(out, mine, core * n, axis)
        return lax.dynamic_update_slice_in_dim(out, theirs, (1 - core) * n, axis)

    def after(v, *deps):
        return lax.optimization_barrier((v,) + deps)[0]

    def gather(v):
        return lax.all_gather(v, GROUP, axis=0, tiled=True)

    def local(x, g, w1, w2, w3, w4):
        ff = w1.shape[1]
        gs = gather(g)
        a1 = nn(x, w1).astype(bf)
        h2 = (nn(gelu(a1), w2) + x.astype(f32)).astype(bf)
        h2s = gather(h2)
        a3 = nn(h2, w3).astype(bf)
        xs = gather(after(x, a3))
        da3 = gelu_grad(a3, nt(g, w4).astype(bf))
        dh2 = (nt(da3, w3) + g.astype(f32)).astype(bf)
        dh2s = gather(dh2)
        da1 = gelu_grad(a1, nt(dh2, w2).astype(bf))
        dx = (nt(da1, w1) + dh2.astype(f32)).astype(bf)

        n34 = ff // ndev
        i34 = lax.axis_index(GROUP) * n34
        w3c = lax.dynamic_slice_in_dim(w3, i34, n34, axis=1)
        w4c = lax.dynamic_slice_in_dim(w4, i34, n34, axis=0)
        h2s = after(h2s, dx)
        a3c = nn(h2s, w3c).astype(bf)
        dw4c = tn(gelu(a3c), gs)
        dw4s = gather(dw4c)
        da3c = gelu_grad(a3c, nt(after(gs, dw4c), w4c).astype(bf))
        dw3c = tn(h2s, da3c) / ndev
        dw3s = lax.all_gather(dw3c, GROUP, axis=0, tiled=False)

        n12 = ff // ncore
        i12 = lax.axis_index("dpc") * n12
        w1c = lax.dynamic_slice_in_dim(w1, i12, n12, axis=1)
        w2c = lax.dynamic_slice_in_dim(w2, i12, n12, axis=0)
        xs = after(xs, dw3c)
        a1c = nn(xs, w1c).astype(bf)
        dw2c = tn(gelu(a1c), dh2s) / ndev
        dw2o = swap(dw2c)
        da1c = gelu_grad(a1c, nt(after(dh2s, dw2c), w2c).astype(bf))
        dw2 = join(dw2c, after(dw2o, da1c), 0)
        da1c, dw4s = lax.optimization_barrier((da1c, dw4s))
        dw4 = dw4s / ndev
        dw1c = tn(xs, after(da1c, dw2, dw4)) / ndev
        dw1o = swap(dw1c)
        dw1 = join(dw1c, dw1o, 1)
        dw3 = jnp.swapaxes(after(dw3s, dw1c), 0, 1).reshape(dw3s.shape[1], ff)
        return dw1, dw2, dw3, dw4, dx

    return jax.shard_map(local, mesh=mesh, in_specs=(rows, rows, wspec, wspec, wspec, wspec), out_specs=(wspec, wspec, wspec, wspec, rows), check_vma=False)
```

time: 3330 us -> 1500 us (0.45)
  waiting for transfers between devices: 2390 us -> 25.3 us
  matrix products: 574 us -> 1260 us
  other arithmetic: 218 us -> 44.3 us
    psum x2 -> x0, waiting for transfers between devices: 2230 us -> none  [reduce_grad(): s = lax.psum(s, ('dpa', 'dpb'))]
    dot_general x11 -> x15, matrix products: 574 us -> 1260 us  [the longest x6 501 us: nt(): lax.dot_general(a, b, (((1,), (1,)), ((), ())), preferred_element_type=f32)]
    div x4 -> x1, other arithmetic: 218 us -> 44.3 us  [local(): dw4 = dw4s / ndev]
    unnamed x4 -> x0, local copies, waits for them, and re-layouts: 129 us -> none
    reduce_scatter x4 -> x0, waiting for transfers between devices: 76.4 us -> none  [reduce_grad(): s = lax.psum_scatter(dw, 'dpc', scatter_dimension=0, tiled=True)]
    all_gather x4 -> x6, waiting for transfers between devices: 80.7 us -> 19.1 us  [the longest x5 19.1 us: gather(): return lax.all_gather(v, GROUP, axis=0, tiled=True)]
    broadcast_in_dim x0 -> x2, local copies, waits for them, and re-layouts: none -> 51.1 us  [join(): out = jnp.zeros(shape, mine.dtype)]
    dynamic_update_slice x0 -> x2, local copies, waits for them, and re-layouts: none -> 50.6 us  [join(): return lax.dynamic_update_slice_in_dim(out, theirs, (1 - core) * n, axis)]
  transfers between devices with their start and end apart: 10 -> 8, of which waited for: 5 -> 3; matrix products, arithmetic and copies ran while one was open for 21% -> 89% of each run, Pallas kernels for 0% -> 0%
where the time goes in v1:
time: 1500 us; the launch traced here: 1490 us
  matrix products  1260 us (84%)
  local copies, waits for them, and re-layouts  145 us (10%)
  other arithmetic  44.3 us (3%)
  waiting for transfers between devices  25.3 us (2%)
    dot_general x6, matrix products, nt(): lax.dot_general(a, b, (((1,), (1,)), ((), ())), preferred_element_type=f32)  501 us
    dot_general x4, matrix products, tn(): lax.dot_general(a, b, (((0,), (0,)), ((), ())), preferred_element_type=f32)  428 us
    dot_general x5, matrix products, nn(): return jnp.dot(a, b, preferred_element_type=f32)  330 us
    broadcast_in_dim x2, local copies, waits for them, and re-layouts, join(): out = jnp.zeros(shape, mine.dtype)  51.1 us
    dynamic_update_slice x2, local copies, waits for them, and re-layouts, join(): return lax.dynamic_update_slice_in_dim(out, theirs, (1 - core) * n, axis)  50.6 us
    div x1, other arithmetic, local(): dw4 = dw4s / ndev  44.3 us
    reshape x1, local copies, waits for them, and re-layouts, local(): dw3 = jnp.swapaxes(after(dw3s, dw1c), 0, 1).reshape(dw3s.shape[1], ff)  43.7 us
  transfers between devices with their start and end apart: 8, of which 3 were waited for; matrix products, arithmetic and copies ran while one was open for 89% of the time, Pallas kernels for 0%

profile of v1, /device:TPU:0, one launch (start us, length us, event | category | flops | bytes accessed | tf_op | source)
XLA Modules:
  0.0 1490.3 jit_solution(5069499136899009669)
XLA Ops:
  7.2 41.9 %convolution_convert_fusion.3 = bf16[1024,8192]{1,0:T(8,128)(2,1)} fusion(bf16[1024,2048]{1,0:T(8,128)(2,1)} %param.6, bf16[2048,8192]{1,0:T(8,128)(2,1)} %param.8), kind=kOutput, calls=%fused_computation.81 | convolution fusion | flops 34368126976 | bytes 54525952 | tf_op jit(solution)/shard_map/dot_general | solution.py:21
  49.1 52.5 %add_convert_fusion.2 = bf16[1024,2048]{1,0:T(8,128)(2,1)} fusion(bf16[1024,2048]{1,0:T(8,128)(2,1)} %param.6, bf16[8192,2048]{1,0:T(8,128)(2,1)} %param.9, bf16[1024,8192]{1,0:T(8,128)(2,1)} %convolution_convert_fusion.3), kind=kOutput, calls=%fused_computation.84 | convolution fusion | flops 34449915904 | bytes 58720256 | tf_op jit(solution)/shard_map/dot_general | solution.py:21
  101.7 0.0 all-gather.12.cloned.1.call-start
  101.7 0.7 all-gather.12.cloned.1.call-update
  102.4 0.0 all-gather.8.cloned.1.call-start
  102.5 42.2 %convolution_convert_fusion.2 = bf16[1024,8192]{1,0:T(8,128)(2,1)} fusion(bf16[1024,2048]{1,0:T(8,128)(2,1)} %add_convert_fusion.2, bf16[2048,8192]{1,0:T(8,128)(2,1)} %param.10), kind=kOutput, calls=%fused_computation.80 | convolution fusion | flops 34368126976 | bytes 54525952 | tf_op jit(solution)/shard_map/dot_general | solution.py:21
  144.6 0.0 all-gather.14.cloned.1.call-start
  144.7 42.3 %fusion.109 = bf16[1024,8192]{1,0:T(8,128)(2,1)} fusion(bf16[1024,2048]{1,0:T(8,128)(2,1)} %param.7, bf16[8192,2048]{1,0:T(8,128)(2,1)} %param.11), kind=kOutput, calls=%fused_computation.126 | convolution fusion | flops 34359738368 | bytes 54525952 | tf_op jit(solution)/shard_map/dot_general | solution.py:25
  187.0 64.3 %add_convert_fusion.1 = bf16[1024,2048]{1,0:T(8,128)(2,1)} fusion(bf16[1024,2048]{1,0:T(8,128)(2,1)} %param.7, bf16[2048,8192]{1,0:T(8,128)(2,1)} %param.10, bf16[1024,8192]{1,0:T(8,128)(2,1)} %convolution_convert_fusion.2, bf16[1024,8192]{1,0:T(8,128)(2,1)} %fusion.109), kind=kOutput, calls=%fused_computation.83 | convolution fusion | flops 34550579200 | bytes 75497472 | tf_op jit(solution)/shard_map/dot_general | solution.py:25
  251.4 0.0 all-gather.16.cloned.1.call-start
  251.4 42.2 %fusion.110 = bf16[1024,8192]{1,0:T(8,128)(2,1)} fusion(bf16[1024,2048]{1,0:T(8,128)(2,1)} %add_convert_fusion.1, bf16[8192,2048]{1,0:T(8,128)(2,1)} %param.9), kind=kOutput, calls=%fused_computation.127 | convolution fusion | flops 34359738368 | bytes 54525952 | tf_op jit(solution)/shard_map/dot_general | solution.py:25
  293.6 63.8 %add_convert_fusion = bf16[1024,2048]{1,0:T(8,128)(2,1)} fusion(bf16[1024,2048]{1,0:T(8,128)(2,1)} %add_convert_fusion.1, bf16[2048,8192]{1,0:T(8,128)(2,1)} %param.8, bf16[1024,8192]{1,0:T(8,128)(2,1)} %convolution_convert_fusion.3, bf16[1024,8192]{1,0:T(8,128)(2,1)} %fusion.110), kind=kOutput, calls=%fused_computation.82 | convolution fusion | flops 34550579200 | bytes 75497472 | tf_op jit(solution)/shard_map/dot_general | solution.py:25
  357.4 41.6 %convolution_convert_fusion.1 = bf16[8192,1024]{1,0:T(8,128)(2,1)} fusion(bf16[8192,2048]{1,0:T(8,128)(2,1)} %all-gather.10.cloned.1.call-done, bf16[2048,8192]{1,0:T(8,128)(2,1)} %param.10, s32[]{:T(128)S(6)} %select_n.6), kind=kOutput, calls=%fused_computation.79 | convolution fusion | flops 34368126976 | bytes 54525956 | tf_op jit(solution)/shard_map/dot_general | solution.py:21
  399.0 17.6 %all-gather.12.cloned.1.call-done = bf16[8192,2048]{1,0:T(8,128)(2,1)} async-done(((bf16[1024,2048]{1,0:T(8,128)(2,1)}), bf16[8192,2048]{1,0:T(8,128)(2,1)}) %all-gather.12.cloned.1.call-update) | async-done | bytes 33554448 | tf_op jit(solution)/shard_map/all_gather | solution.py:54
  416.7 50.6 %fusion.50 = f32[1024,2048]{1,0:T(8,128)} fusion(bf16[8192,2048]{1,0:T(8,128)(2,1)} %all-gather.12.cloned.1.call-done, bf16[8192,1024]{1,0:T(8,128)(2,1)} %convolution_convert_fusion.1), kind=kOutput, calls=%fused_computation.73 | convolution fusion | flops 34443624448 | bytes 58720256 | tf_op jit(solution)/shard_map/dot_general | solution.py:29
  467.3 0.0 all-gather.18.cloned.1.call-start
  467.4 64.6 %fusion.150 = bf16[8192,1024]{1,0:T(8,128)(2,1)} fusion(bf16[8192,1024]{1,0:T(8,128)(2,1)} %convolution_convert_fusion.1, bf16[8192,2048]{1,0:T(8,128)(2,1)} %all-gather.12.cloned.1.call-done, bf16[8192,2048]{1,0:T(8,128)(2,1)} %param.11, s32[]{:T(128)S(6)} %select_n.6), kind=kOutput, calls=%fused_computation.47.clone.clone.clone.clone.1 | convolution fusion | flops 34552676352 | bytes 71303168 | tf_op jit(solution)/shard_map/dot_general | solution.py:25
  532.0 44.8 %fusion.62 = f32[2048,1024]{1,0:T(8,128)} fusion(bf16[8192,2048]{1,0:T(8,128)(2,1)} %all-gather.10.cloned.1.call-done, bf16[8192,1024]{1,0:T(8,128)(2,1)} %fusion.150), kind=kOutput, calls=%fused_computation.85 | convolution fusion | flops 34361835520 | bytes 58720256 | tf_op jit(solution)/shard_map/dot_general | solution.py:29
  576.8 152.1 %convolution_convert_fusion = bf16[8192,4096]{1,0:T(8,128)(2,1)} fusion(bf16[8192,2048]{1,0:T(8,128)(2,1)} %all-gather.8.cloned.1.call-done, bf16[2048,8192]{1,0:T(8,128)(2,1)} %param.8, s32[]{:T(128)S(6)} %select_n.7), kind=kOutput, calls=%fused_computation.28 | convolution fusion | flops 137472507904 | bytes 117440512 | tf_op jit(solution)/shard_map/dot_general | solution.py:21
  728.9 1.5 all-gather.14.cloned.1.call-done
  730.4 29.3 %broadcast_in_dim.7 = f32[8192,2048]{1,0:T(8,128)} broadcast(f32[]{:T(128)} %constant.17.clone.1), dimensions={} | broadcast | bytes 67108864 | tf_op jit(solution)/shard_map/broadcast_in_dim | solution.py:46
  759.7 162.2 %constant_dynamic-update-slice_fusion.3 = (f32[8192,2048]{1,0:T(8,128)}, f32[4096,2048]{1,0:T(8,128)}) fusion(f32[8192,2048]{1,0:T(8,128)} %broadcast_in_dim.7, s32[]{:T(128)S(6)} %select_n.7, bf16[8192,2048]{1,0:T(8,128)(2,1)} %all-gather.14.cloned.1.call-done, bf16[8192,4096]{1,0:T(8,128)(2,1)} %convolution_convert_fusion), kind=kOutput, calls=%fused_computation.91 | convolution fusion | flops 137782886400 | bytes 167772160 | tf_op jit(solution)/shard_map/dot_general | solution.py:29
  921.9 0.3 collective-permute-start
  922.2 223.6 %fusion.3 = bf16[8192,4096]{1,0:T(8,128)(2,1)} fusion(bf16[8192,4096]{1,0:T(8,128)(2,1)} %convolution_convert_fusion, bf16[8192,2048]{1,0:T(8,128)(2,1)} %all-gather.14.cloned.1.call-done, bf16[8192,2048]{1,0:T(8,128)(2,1)} %param.9, s32[]{:T(128)S(6)} %select_n.7), kind=kOutput, calls=%fused_computation.9 | convolution fusion | flops 138210705408 | bytes 184549376 | tf_op jit(solution)/shard_map/dot_general | solution.py:25
  1145.8 27.6 %constant_dynamic-update-slice_fusion.2 = f32[8192,2048]{1,0:T(8,128)} fusion(f32[8192,2048]{1,0:T(8,128)} %get-tuple-element.25, f32[4096,2048]{1,0:T(8,128)} %collective-permute-done, s32[]{:T(128)S(6)} %select_n.16), kind=kLoop, calls=%fused_computation.90 | loop fusion | bytes 67108864 | tf_op jit(solution)/shard_map/dynamic_update_slice | solution.py:48
  1173.5 44.3 %broadcast_multiply_fusion = f32[8192,2048]{1,0:T(8,128)} fusion(f32[8192,2048]{1,0:T(8,128)} %all-gather.16.cloned.1.call-done), kind=kLoop, calls=%fused_computation.68 | loop fusion | flops 16777216 | bytes 134217728 | tf_op jit(solution)/shard_map/div | solution.py:93
  1217.8 21.8 %broadcast_in_dim.6 = f32[2048,8192]{1,0:T(8,128)} broadcast(f32[]{:T(128)} %constant.17.clone.1), dimensions={} | broadcast | bytes 67108864 | tf_op jit(solution)/shard_map/broadcast_in_dim | solution.py:46
  1239.6 170.0 %constant_dynamic-update-slice_fusion.1 = (f32[2048,8192]{1,0:T(8,128)}, f32[2048,4096]{1,0:T(8,128)}) fusion(f32[2048,8192]{1,0:T(8,128)} %broadcast_in_dim.6, s32[]{:T(128)S(6)} %select_n.7, bf16[8192,2048]{1,0:T(8,128)(2,1)} %all-gather.8.cloned.1.call-done, bf16[8192,4096]{1,0:T(8,128)(2,1)} %fusion.3), kind=kOutput, calls=%fused_computation.89 | convolution fusion | flops 137447342080 | bytes 167772160 | tf_op jit(solution)/shard_map/dot_general | solution.py:29
  1409.6 1.2 collective-permute-start.1
  1410.8 43.7 %copy.12 = f32[8,256,8,1024]{3,2,0,1:T(8,128)} copy(f32[8,256,8,1024]{3,2,1,0:T(8,128)} %bitcast.2) | data formatting | bytes 134217728 | tf_op jit(solution)/shard_map/reshape | solution.py:97
  1454.6 5.4 collective-permute-done.1
  1459.9 23.0 %constant_dynamic-update-slice_fusion = f32[2048,8192]{1,0:T(8,128)} fusion(f32[2048,8192]{1,0:T(8,128)} %get-tuple-element.27, f32[2048,4096]{1,0:T(8,128)} %collective-permute-done.1, s32[]{:T(128)S(6)} %select_n.16), kind=kLoop, calls=%fused_computation.88 | loop fusion | bytes 67108864 | tf_op jit(solution)/shard_map/dynamic_update_slice | solution.py:48
  (11 shorter events, 0.1 us)
Async XLA Ops:
  7.2 350.3 %all-gather.10.cloned.1.call-start = ((), (), s32[]{:S(2)}) async-start(), calls=%async_computation.1 | async-start | bytes 37748736 | tf_op jit(solution)/shard_map/all_gather | solution.py:54
  101.7 315.0 %all-gather.12.cloned.1.call-start = ((), (), s32[]{:S(2)}) async-start(), calls=%async_computation.2 | async-start | bytes 37748736 | tf_op jit(solution)/shard_map/all_gather | solution.py:54
  102.4 474.4 %all-gather.8.cloned.1.call-start = ((), (), s32[]{:S(2)}) async-start(), calls=%async_computation | async-start | bytes 37748736 | tf_op jit(solution)/shard_map/all_gather | solution.py:54
  144.6 585.8 %all-gather.14.cloned.1.call-start = ((), (), s32[]{:S(2)}) async-start(), calls=%async_computation.3 | async-start | bytes 37748736 | tf_op jit(solution)/shard_map/all_gather | solution.py:54
  251.4 922.1 %all-gather.16.cloned.1.call-start = ((), (), s32[]{:S(2)}) async-start(), calls=%async_computation.4 | async-start | bytes 75497472 | tf_op jit(solution)/shard_map/all_gather | solution.py:54
  467.3 943.5 %all-gather.18.cloned.1.call-start = ((), (), s32[]{:S(2)}) async-start(), calls=%async_computation.5 | async-start | bytes 75497472 | tf_op jit(solution)/shard_map/all_gather | solution.py:80
  921.9 223.9 %collective-permute-start = (f32[4096,2048]{1,0:T(8,128)}, f32[4096,2048]{1,0:T(8,128)}, u32[]{:S(2)}, u32[]{:S(2)}) collective-permute-start(f32[4096,2048]{1,0:T(8,128)} %get-tuple-element.26), channel_id=1, source_target_pairs={{0,1},{1,0},{2,3},{3,2},{4,5},{5,4},{6,7},{7,6}} | collective-permute-start | bytes 100663304 | tf_op jit(solution)/shard_map/ppermute | solution.py:39
  1409.6 50.3 %collective-permute-start.1 = (f32[2048,4096]{1,0:T(8,128)}, f32[2048,4096]{1,0:T(8,128)}, u32[]{:S(2)}, u32[]{:S(2)}) collective-permute-start(f32[2048,4096]{1,0:T(8,128)} %get-tuple-element.28), channel_id=1, source_target_pairs={{0,1},{1,0},{2,3},{3,2},{4,5},{5,4},{6,7},{7,6}} | collective-permute-start | bytes 100663304 | tf_op jit(solution)/shard_map/ppermute | solution.py:39
Sparse Core Ops, SparseCore 0:
  101.8 157.8 all-gather.9
  261.5 155.0 all-gather.11
  418.5 155.0 all-gather.7
  575.3 155.0 all-gather.13
  732.1 297.1 all-gather.15
  1030.9 297.1 all-gather.17

commit v2 on v1

v2 whole, which is shorter than its diff:
```python
import functools
import math

import jax
import jax.numpy as jnp
from jax import lax
from jax.experimental import pallas as pl
from jax.experimental.pallas import tpu as pltpu
from jax.sharding import PartitionSpec as P


GROUP = ("dpa", "dpb", "dpc")
f32 = jnp.float32
bf = jnp.bfloat16


def gelu(a):
    return jax.nn.gelu(a.astype(f32), approximate=True).astype(bf)


C0 = (2.0 / math.pi) ** 0.5
C1 = 0.044715 * C0


def grad_kernel(sub, off_ref, d_ref, w_ref, a_ref, o_ref):
    for i in range(d_ref.shape[0] // sub):
        at = pl.ds(i * sub, sub)
        y = nt(d_ref[at, :], w_ref[...]).astype(bf).astype(f32)
        a = a_ref[at, :].astype(f32)
        sq = a * a
        t = jnp.tanh(a * (C0 + C1 * sq))
        h = 0.5 + 0.5 * t
        slope = h + ((h * (1.0 - t)) * a) * (C0 + 3.0 * C1 * sq)
        o_ref[at, :] = (y * slope).astype(bf)


def nt_gelu_grad(d, w, a, first=None, bm=2048, bn=512, sub=512):
    m, k = d.shape
    n = a.shape[1]
    if m < bm:
        bm, bn = m, bm * bn // m
    off = jnp.zeros((1,), jnp.int32) if first is None else (first // bn).astype(jnp.int32).reshape(1)
    return pl.pallas_call(
        functools.partial(grad_kernel, sub),
        out_shape=jax.ShapeDtypeStruct((m, n), bf),
        grid_spec=pltpu.PrefetchScalarGridSpec(
            num_scalar_prefetch=1,
            grid=(m // bm, n // bn),
            in_specs=[
                pl.BlockSpec((bm, k), lambda i, j, o: (i, 0)),
                pl.BlockSpec((bn, k), lambda i, j, o: (j + o[0], 0)),
                pl.BlockSpec((bm, bn), lambda i, j, o: (i, j)),
            ],
            out_specs=pl.BlockSpec((bm, bn), lambda i, j, o: (i, j)),
        ),
        cost_estimate=pl.CostEstimate(flops=2 * m * n * k, bytes_accessed=2 * (m * k + n * k + 2 * m * n), transcendentals=m * n),
        name="nt_gelu_grad",
    )(off, d, w, a)


def place_kernel(p_ref, full_ref, o_ref):
    o_ref[...] = p_ref[...]


def place(full, parts, row, rows=256):
    n, m, width = parts.shape
    return pl.pallas_call(
        place_kernel,
        out_shape=jax.ShapeDtypeStruct(full.shape, full.dtype),
        grid=(m // rows, n),
        in_specs=[pl.BlockSpec((None, rows, width), lambda i, d: (d, i, 0)), pl.BlockSpec(memory_space=pl.ANY)],
        out_specs=pl.BlockSpec((rows, width), lambda i, d: (row // rows + i, d)),
        input_output_aliases={1: 0},
        cost_estimate=pl.CostEstimate(flops=n * m * width, bytes_accessed=8 * n * m * width, transcendentals=0),
        name="place",
    )(parts, full)


def empty(shape, dtype):
    return pl.pallas_call(
        lambda o_ref: None,
        out_shape=jax.ShapeDtypeStruct(shape, dtype),
        out_specs=pl.BlockSpec(memory_space=pl.ANY),
        name="empty",
    )()


def nn(a, b):
    return jnp.dot(a, b, preferred_element_type=f32)


def nt(a, b):
    return lax.dot_general(a, b, (((1,), (1,)), ((), ())), preferred_element_type=f32)


def tn(a, b):
    return lax.dot_general(a, b, (((0,), (0,)), ((), ())), preferred_element_type=f32)


def solution(mesh):
    ndev = mesh.shape["dpa"] * mesh.shape["dpb"] * mesh.shape["dpc"]
    ncore = mesh.shape["dpc"]
    rows = P(("mp",) + GROUP, None)
    wspec = P("mp", None)

    def swap(v):
        return lax.ppermute(v, "dpc", [(i, ncore - 1 - i) for i in range(ncore)])

    def join(mine, theirs, axis):
        core = lax.axis_index("dpc")
        n = mine.shape[axis]
        shape = list(mine.shape)
        shape[axis] = 2 * n
        out = empty(shape, mine.dtype)
        out = lax.dynamic_update_slice_in_dim(out, mine, core * n, axis)
        return lax.dynamic_update_slice_in_dim(out, theirs, (1 - core) * n, axis)

    def after(v, *deps):
        return lax.optimization_barrier((v,) + deps)[0]

    def gather(v, tiled=True):
        return lax.all_gather(v, GROUP, axis=0, tiled=tiled)

    def local(x, g, w1, w2, w3, w4):
        ff = w1.shape[1]
        gs = gather(g)
        a1 = nn(x, w1).astype(bf)
        h2 = (nn(gelu(a1), w2) + x.astype(f32)).astype(bf)
        h2s = gather(h2)
        a3 = nn(h2, w3).astype(bf)
        xs = gather(after(x, a3))
        da3 = nt_gelu_grad(g, w4, a3)
        dh2 = (nt(da3, w3) + g.astype(f32)).astype(bf)
        dh2s = gather(dh2)
        da1 = nt_gelu_grad(dh2, w2, a1)
        dx = (nt(da1, w1) + dh2.astype(f32)).astype(bf)

        n34 = ff // ndev
        i34 = lax.axis_index(GROUP) * n34
        w3c = lax.dynamic_slice_in_dim(w3, i34, n34, axis=1)
        h2s = after(h2s, dx)
        a3c = nn(h2s, w3c).astype(bf)
        dw4c = tn(gelu(a3c), gs)
        dw4s = gather(dw4c)
        da3c = nt_gelu_grad(after(gs, dw4c), w4, a3c, i34)
        dw3c = tn(h2s, da3c) / ndev
        half = dw3c.shape[0] // 2
        dw3s = [gather(dw3c[i * half : (i + 1) * half], False) for i in range(2)]

        n12 = ff // ncore
        i12 = lax.axis_index("dpc") * n12
        w1c = lax.dynamic_slice_in_dim(w1, i12, n12, axis=1)
        xs = after(xs, dw3c)
        a1c = nn(xs, w1c).astype(bf)
        dw2c = tn(gelu(a1c), dh2s) / ndev
        dw2o = swap(dw2c)
        da1c = nt_gelu_grad(after(dh2s, dw2c), w2, a1c, i12)
        dw2 = join(dw2c, after(dw2o, da1c), 0)
        da1c, dw4s = lax.optimization_barrier((da1c, dw4s))
        dw4 = dw4s / ndev
        dw1c = tn(xs, after(da1c, dw2, dw4)) / ndev
        dw1o = swap(dw1c)
        dw3 = empty((dw3c.shape[0], ff), f32)
        for i in range(2):
            dw3 = place(dw3, after(dw3s[i], dw1c, dw3), i * half)
        dw1 = join(dw1c, dw1o, 1)
        return dw1, dw2, dw3, dw4, dx

    return jax.shard_map(local, mesh=mesh, in_specs=(rows, rows, wspec, wspec, wspec, wspec), out_specs=(wspec, wspec, wspec, wspec, rows), check_vma=False)
```

time: 1500 us -> 1460 us (0.973)
  Pallas kernels: 0 us -> 446 us
  matrix products: 1260 us -> 861 us
  local copies, waits for them, and re-layouts: 145 us -> 56 us
    pallas_call x0 -> x9, Pallas kernels: none -> 446 us  [the longest x4 377 us: nt_gelu_grad(): pl.pallas_call(functools.partial(grad_kernel, sub), out_shape=jax.ShapeDt...]
    dot_general x6 -> x2, matrix products: 501 us -> 90.5 us  [nt(): lax.dot_general(a, b, (((1,), (1,)), ((), ())), preferred_element_type=f32)]
    broadcast_in_dim x2 -> x0, local copies, waits for them, and re-layouts: 51.1 us -> none  [join(): out = jnp.zeros(shape, mine.dtype)]
    reshape x1 -> x0, local copies, waits for them, and re-layouts: 43.7 us -> none  [local(): dw3 = jnp.swapaxes(after(dw3s, dw1c), 0, 1).reshape(dw3s.shape[1], ff)]
    all_gather x6 -> x7, waiting for transfers between devices: 19.1 us -> 30.6 us  [gather(): return lax.all_gather(v, GROUP, axis=0, tiled=tiled)]
  transfers between devices with their start and end apart: 8 -> 9, of which waited for: 3 -> 2; matrix products, arithmetic and copies ran while one was open for 89% -> 58% of each run, Pallas kernels for 0% -> 31%
where the time goes in v2:
time: 1460 us; the launch traced here: 1450 us
  matrix products  861 us (59%)
  Pallas kernels  446 us (31%)
  local copies, waits for them, and re-layouts  56 us (4%)
  other arithmetic  44.2 us (3%)
  waiting for transfers between devices  31.4 us (2%)
    dot_general x4, matrix products, tn(): lax.dot_general(a, b, (((0,), (0,)), ((), ())), preferred_element_type=f32)  440 us
    pallas_call x4, Pallas kernels, nt_gelu_grad(): pl.pallas_call(functools.partial(grad_kernel, sub), out_shape=jax.ShapeDt...  377 us
    dot_general x5, matrix products, nn(): return jnp.dot(a, b, preferred_element_type=f32)  331 us
    dot_general x2, matrix products, nt(): lax.dot_general(a, b, (((1,), (1,)), ((), ())), preferred_element_type=f32)  90.5 us
    pallas_call x2, Pallas kernels, place(): pl.pallas_call(place_kernel, out_shape=jax.ShapeDtypeStruct(full.shape, f...  68.8 us
    dynamic_update_slice x2, local copies, waits for them, and re-layouts, join(): return lax.dynamic_update_slice_in_dim(out, theirs, (1 - core) * n, axis)  46.3 us
    div x1, other arithmetic, local(): dw4 = dw4s / ndev  44.2 us
    all_gather x7, waiting for transfers between devices, gather(): return lax.all_gather(v, GROUP, axis=0, tiled=tiled)  30.6 us
  transfers between devices with their start and end apart: 9, of which 2 were waited for; matrix products, arithmetic and copies ran while one was open for 58% of the time, Pallas kernels for 31%

profile of v2, /device:TPU:0, one launch (start us, length us, event | category | flops | bytes accessed | tf_op | source)
XLA Modules:
  0.0 1454.8 jit_solution(12444671124628638569)
XLA Ops:
  7.2 0.0 all-gather.12.cloned.1.call-start
  7.2 41.9 %convolution_convert_fusion.3.a_ref = bf16[1024,8192]{1,0:T(8,128)(2,1)} fusion(bf16[1024,2048]{1,0:T(8,128)(2,1)} %param.6, bf16[2048,8192]{1,0:T(8,128)(2,1)} %param.8), kind=kOutput, calls=%fused_computation.40 | convolution fusion | flops 34368126976 | bytes 54525952 | tf_op jit(solution)/shard_map/dot_general | solution.py:89
  49.1 52.8 %add_convert_fusion.2 = bf16[1024,2048]{1,0:T(8,128)(2,1)} fusion(bf16[1024,2048]{1,0:T(8,128)(2,1)} %param.6, bf16[8192,2048]{1,0:T(8,128)(2,1)} %w_ref.7, bf16[1024,8192]{1,0:T(8,128)(2,1)} %convolution_convert_fusion.3.a_ref), kind=kOutput, calls=%fused_computation.43 | convolution fusion | flops 34449915904 | bytes 58720256 | tf_op jit(solution)/shard_map/dot_general | solution.py:89
  102.0 0.0 all-gather.14.cloned.1.call-start
  102.0 0.7 all-gather.14.cloned.1.call-update
  102.8 42.1 %convolution_convert_fusion.2.a_ref = bf16[1024,8192]{1,0:T(8,128)(2,1)} fusion(bf16[1024,2048]{1,0:T(8,128)(2,1)} %add_convert_fusion.2, bf16[2048,8192]{1,0:T(8,128)(2,1)} %param.10), kind=kOutput, calls=%fused_computation.39 | convolution fusion | flops 34368126976 | bytes 54525952 | tf_op jit(solution)/shard_map/dot_general | solution.py:89
  144.9 0.0 all-gather.16.cloned.1.call-start
  144.9 55.4 %nt_gelu_grad.4 = bf16[1024,8192]{1,0:T(8,128)(2,1)} custom-call(s32[1]{0:T(128)} %constant.28.clone.1.off_ref, bf16[1024,2048]{1,0:T(8,128)(2,1)} %d_ref.1, bf16[8192,2048]{1,0:T(8,128)(2,1)} %w_ref.6, bf16[1024,8192]{1,0:T(8,128)(2,1)} %convolution_convert_fusion.2.a_ref), custom_call_target="tpu_custom_call" | custom-call | flops 34359738368 | bytes 71303168 | tf_op jit(solution)/shard_map/nt_gelu_grad/pallas_call | solution.py:43
  200.3 45.3 %add_convert_fusion.1.d_ref = bf16[1024,2048]{1,0:T(8,128)(2,1)} fusion(bf16[1024,2048]{1,0:T(8,128)(2,1)} %d_ref.1, bf16[1024,8192]{1,0:T(8,128)(2,1)} %nt_gelu_grad.4, bf16[2048,8192]{1,0:T(8,128)(2,1)} %param.10), kind=kOutput, calls=%fused_computation.42 | convolution fusion | flops 34366029824 | bytes 58720256 | tf_op jit(solution)/shard_map/dot_general | solution.py:93
  245.6 0.0 all-gather.18.cloned.1.call-start
  245.7 55.6 %nt_gelu_grad.5 = bf16[1024,8192]{1,0:T(8,128)(2,1)} custom-call(s32[1]{0:T(128)} %constant.28.clone.1.off_ref, bf16[1024,2048]{1,0:T(8,128)(2,1)} %add_convert_fusion.1.d_ref, bf16[8192,2048]{1,0:T(8,128)(2,1)} %w_ref.7, bf16[1024,8192]{1,0:T(8,128)(2,1)} %convolution_convert_fusion.3.a_ref), custom_call_target="tpu_custom_call" | custom-call | flops 34359738368 | bytes 71303168 | tf_op jit(solution)/shard_map/nt_gelu_grad/pallas_call | solution.py:43
  301.3 45.2 %add_convert_fusion = bf16[1024,2048]{1,0:T(8,128)(2,1)} fusion(bf16[1024,2048]{1,0:T(8,128)(2,1)} %add_convert_fusion.1.d_ref, bf16[1024,8192]{1,0:T(8,128)(2,1)} %nt_gelu_grad.5, bf16[2048,8192]{1,0:T(8,128)(2,1)} %param.8), kind=kOutput, calls=%fused_computation.41 | convolution fusion | flops 34366029824 | bytes 58720256 | tf_op jit(solution)/shard_map/dot_general | solution.py:93
  346.5 42.1 %convolution_convert_fusion.1.a_ref = bf16[8192,1024]{1,0:T(8,128)(2,1)} fusion(bf16[8192,2048]{1,0:T(8,128)(2,1)} %all-gather.12.cloned.1.call-done, bf16[2048,8192]{1,0:T(8,128)(2,1)} %param.10, s32[]{:T(128)S(6)} %select_n.21), kind=kOutput, calls=%fused_computation.38 | convolution fusion | flops 34368126976 | bytes 54525956 | tf_op jit(solution)/shard_map/dot_general | solution.py:89
  388.6 28.4 %all-gather.14.cloned.1.call-done.d_ref = bf16[8192,2048]{1,0:T(8,128)(2,1)} async-done(((bf16[1024,2048]{1,0:T(8,128)(2,1)}), bf16[8192,2048]{1,0:T(8,128)(2,1)}) %all-gather.14.cloned.1.call-update) | async-done | bytes 33554448 | tf_op jit(solution)/shard_map/all_gather | solution.py:122
  417.0 50.5 %fusion.24 = f32[1024,2048]{1,0:T(8,128)} fusion(bf16[8192,2048]{1,0:T(8,128)(2,1)} %all-gather.14.cloned.1.call-done.d_ref, bf16[8192,1024]{1,0:T(8,128)(2,1)} %convolution_convert_fusion.1.a_ref), kind=kOutput, calls=%fused_computation.36 | convolution fusion | flops 34443624448 | bytes 58720256 | tf_op jit(solution)/shard_map/dot_general | solution.py:97
  467.5 0.0 all-gather.22.cloned.1.call-start
  467.6 59.3 %nt_gelu_grad.6 = bf16[8192,1024]{1,0:T(8,128)(2,1)} custom-call(s32[1]{0:T(128)} %bitcast.off_ref, bf16[8192,2048]{1,0:T(8,128)(2,1)} %all-gather.14.cloned.1.call-done.d_ref, bf16[8192,2048]{1,0:T(8,128)(2,1)} %w_ref.6, bf16[8192,1024]{1,0:T(8,128)(2,1)} %convolution_convert_fusion.1.a_ref), custom_call_target="tpu_custom_call" | custom-call | flops 34359738368 | bytes 71303168 | tf_op jit(solution)/shard_map/nt_gelu_grad/pallas_call | solution.py:43
  526.9 44.9 %convolution_multiply_fusion.1 = f32[2048,1024]{1,0:T(8,128)} fusion(bf16[8192,2048]{1,0:T(8,128)(2,1)} %all-gather.12.cloned.1.call-done, bf16[8192,1024]{1,0:T(8,128)(2,1)} %nt_gelu_grad.6), kind=kOutput, calls=%fused_computation.44 | convolution fusion | flops 34361835520 | bytes 58720256 | tf_op jit(solution)/shard_map/dot_general | solution.py:97
  571.8 2.1 all-gather.10.cloned.1.call-done
  573.9 9.7 fusion.45
  583.7 151.7 %convolution_convert_fusion.a_ref = bf16[8192,4096]{1,0:T(8,128)(2,1)} fusion(bf16[8192,2048]{1,0:T(8,128)(2,1)} %all-gather.10.cloned.1.call-done, bf16[2048,8192]{1,0:T(8,128)(2,1)} %param.8, s32[]{:T(128)S(6)} %select_n.23), kind=kOutput, calls=%fused_computation.11 | convolution fusion | flops 137472507904 | bytes 117440512 | tf_op jit(solution)/shard_map/dot_general | solution.py:89
  735.4 0.0 all-gather.20.cloned.1.call-start
  735.4 170.4 %constant_dynamic-update-slice_fusion.3 = (f32[8192,2048]{1,0:T(8,128)}, f32[4096,2048]{1,0:T(8,128)}) fusion(f32[8192,2048]{1,0:T(8,128)} %empty.4, s32[]{:T(128)S(6)} %select_n.23, bf16[8192,2048]{1,0:T(8,128)(2,1)} %all-gather.16.cloned.1.call-done.d_ref, bf16[8192,4096]{1,0:T(8,128)(2,1)} %convolution_convert_fusion.a_ref), kind=kOutput, calls=%fused_computation.49 | convolution fusion | flops 137782886400 | bytes 167772160 | tf_op jit(solution)/shard_map/dot_general | solution.py:97
  905.8 0.5 collective-permute-start
  906.3 206.9 %nt_gelu_grad.7 = bf16[8192,4096]{1,0:T(8,128)(2,1)} custom-call(s32[1]{0:T(128)} %bitcast.1.off_ref, bf16[8192,2048]{1,0:T(8,128)(2,1)} %all-gather.16.cloned.1.call-done.d_ref, bf16[8192,2048]{1,0:T(8,128)(2,1)} %w_ref.7, bf16[8192,4096]{1,0:T(8,128)(2,1)} %convolution_convert_fusion.a_ref), custom_call_target="tpu_custom_call" | custom-call | flops 137438953472 | bytes 184549376 | tf_op jit(solution)/shard_map/nt_gelu_grad/pallas_call | solution.py:43
  1113.2 23.3 %constant_dynamic-update-slice_fusion.2 = f32[8192,2048]{1,0:T(8,128)} fusion(f32[8192,2048]{1,0:T(8,128)} %get-tuple-element.29, f32[4096,2048]{1,0:T(8,128)} %collective-permute-done, s32[]{:T(128)S(6)} %select_n.24), kind=kLoop, calls=%fused_computation.48 | loop fusion | bytes 67108864 | tf_op jit(solution)/shard_map/dynamic_update_slice | solution.py:116
  1136.5 44.2 %broadcast_multiply_fusion = f32[8192,2048]{1,0:T(8,128)} fusion(f32[8192,2048]{1,0:T(8,128)} %all-gather.18.cloned.1.call-done), kind=kLoop, calls=%fused_computation.32 | loop fusion | flops 16777216 | bytes 134217728 | tf_op jit(solution)/shard_map/div | solution.py:160
  1180.7 173.9 %constant_dynamic-update-slice_fusion.1 = (f32[2048,8192]{1,0:T(8,128)}, f32[2048,4096]{1,0:T(8,128)}) fusion(f32[2048,8192]{1,0:T(8,128)} %empty.3, s32[]{:T(128)S(6)} %select_n.23, bf16[8192,2048]{1,0:T(8,128)(2,1)} %all-gather.10.cloned.1.call-done, bf16[8192,4096]{1,0:T(8,128)(2,1)} %nt_gelu_grad.7), kind=kOutput, calls=%fused_computation.47 | convolution fusion | flops 137447342080 | bytes 167772160 | tf_op jit(solution)/shard_map/dot_general | solution.py:97
  1354.6 1.3 collective-permute-start.1
  1355.9 34.3 %place.2.full_ref = f32[2048,8192]{1,0:T(8,128)} custom-call(f32[8,1024,1024]{2,1,0:T(8,128)} %bitcast.23, f32[2048,8192]{1,0:T(8,128)} %empty.5.full_ref), custom_call_target="tpu_custom_call", output_to_operand_aliasing={{}: (1, {})} | custom-call | flops 8388608 | bytes 67108864 | tf_op jit(solution)/shard_map/place/pallas_call | solution.py:67
  1390.2 34.4 %place.3 = f32[2048,8192]{1,0:T(8,128)} custom-call(f32[8,1024,1024]{2,1,0:T(8,128)} %bitcast.24, f32[2048,8192]{1,0:T(8,128)} %place.2.full_ref), custom_call_target="tpu_custom_call", output_to_operand_aliasing={{}: (1, {})} | custom-call | flops 8388608 | bytes 67108864 | tf_op jit(solution)/shard_map/place/pallas_call | solution.py:67
  1424.7 23.0 %constant_dynamic-update-slice_fusion = f32[2048,8192]{1,0:T(8,128)} fusion(f32[2048,8192]{1,0:T(8,128)} %get-tuple-element.31, f32[2048,4096]{1,0:T(8,128)} %collective-permute-done.1, s32[]{:T(128)S(6)} %select_n.24), kind=kLoop, calls=%fused_computation.46 | loop fusion | bytes 67108864 | tf_op jit(solution)/shard_map/dynamic_update_slice | solution.py:116
  (17 shorter events, 0.2 us)
Async XLA Ops:
  7.2 339.3 %all-gather.12.cloned.1.call-start = ((), (), s32[]{:S(2)}) async-start(), calls=%async_computation.1 | async-start | bytes 37748736 | tf_op jit(solution)/shard_map/all_gather | solution.py:122
  102.0 315.0 %all-gather.14.cloned.1.call-start = ((), (), s32[]{:S(2)}) async-start(), calls=%async_computation.2 | async-start | bytes 37748736 | tf_op jit(solution)/shard_map/all_gather | solution.py:122
  102.7 471.2 %all-gather.10.cloned.1.call-start = ((), (), s32[]{:S(2)}) async-start(), calls=%async_computation | async-start | bytes 37748736 | tf_op jit(solution)/shard_map/all_gather | solution.py:122
  144.9 590.6 %all-gather.16.cloned.1.call-start = ((), (), s32[]{:S(2)}) async-start(), calls=%async_computation.3 | async-start | bytes 37748736 | tf_op jit(solution)/shard_map/all_gather | solution.py:122
  245.6 890.8 %all-gather.18.cloned.1.call-start = ((), (), s32[]{:S(2)}) async-start(), calls=%async_computation.4 | async-start | bytes 75497472 | tf_op jit(solution)/shard_map/all_gather | solution.py:122
  467.5 888.4 %all-gather.22.cloned.1.call-start = ((), (), s32[]{:S(2)}) async-start(), calls=%async_computation.6 | async-start | bytes 37748736 | tf_op jit(solution)/shard_map/all_gather | solution.py:122
  735.4 654.9 %all-gather.20.cloned.1.call-start = ((), (), s32[]{:S(2)}) async-start(), calls=%async_computation.5 | async-start | bytes 37748736 | tf_op jit(solution)/shard_map/all_gather | solution.py:122
  905.8 207.4 %collective-permute-start = (f32[4096,2048]{1,0:T(8,128)}, f32[4096,2048]{1,0:T(8,128)}, u32[]{:S(2)}, u32[]{:S(2)}) collective-permute-start(f32[4096,2048]{1,0:T(8,128)} %get-tuple-element.30), channel_id=1, source_target_pairs={{0,1},{1,0},{2,3},{3,2},{4,5},{5,4},{6,7},{7,6}} | collective-permute-start | bytes 100663304 | tf_op jit(solution)/shard_map/ppermute | solution.py:107
  1354.6 70.0 %collective-permute-start.1 = (f32[2048,4096]{1,0:T(8,128)}, f32[2048,4096]{1,0:T(8,128)}, u32[]{:S(2)}, u32[]{:S(2)}) collective-permute-start(f32[2048,4096]{1,0:T(8,128)} %get-tuple-element.32), channel_id=1, source_target_pairs={{0,1},{1,0},{2,3},{3,2},{4,5},{5,4},{6,7},{7,6}} | collective-permute-start | bytes 100663304 | tf_op jit(solution)/shard_map/ppermute | solution.py:107
Sparse Core Ops, SparseCore 0:
  102.1 157.8 all-gather.11
  261.8 155.0 all-gather.13
  418.8 155.0 all-gather.9
  575.6 155.0 all-gather.15
  732.4 297.1 all-gather.17
  1031.2 155.0 all-gather.21
  1188.2 155.0 all-gather.19
